TPU v7x, 32 devices: a whole 2x2x4 slice. The times are simulated.
32 devices in a mesh: gx: 8 (over z, core), gy: 4 (over y, x).
Axes of the slice: x: 2, y: 2, z: 4, core: 2. Of those that a mesh axis runs over, the one named last changes fastest.
Arguments:
- velocity: float32 [3, 32, 32, 128], P(None, 'gx', 'gy'), may hold values from -4 to 4
- forcing: float32 [3, 32, 32, 128], P(None, 'gx', 'gy'), may hold values from -6 to 6
- viscosity: float32 [32, 32, 128], P('gx', 'gy'), may hold values from 0.05 to 0.5
- residual_prev: float32 [3, 32, 32, 128], P(None, 'gx', 'gy'), may hold values from -4 to 4
- value_prev: float32 [3, 32, 32, 128], P(None, 'gx', 'gy'), may hold values from -4 to 4
- hist_res: float32 [5, 3, 32, 32, 128], P(None, None, 'gx', 'gy'), may hold values from -16 to 16
- hist_val: float32 [5, 3, 32, 32, 128], P(None, None, 'gx', 'gy'), may hold values from -4 to 4
Outputs:
- velocity_out: float32 [3, 32, 32, 128], P(None, 'gx', 'gy')
- residual_out: float32 [3, 32, 32, 128], P(None, 'gx', 'gy')
All inputs are finite; a program needn't handle non-finite values.
Results may differ from a plain program's by a relative error of at most 0.0003.
Values sent between devices are 32-bit elements; how exact they have to be, the bound alone decides.
A program may use at most 64 MiB of HBM per device.

v0:
```python
import functools

import jax
import jax.numpy as jnp
from jax import lax
from jax.experimental import pallas as pl
from jax.experimental.pallas import tpu as pltpu
from jax.sharding import PartitionSpec as P

SWEEPS = 3
REG = 0.05
FLOOR = 0.001
MESH = pl.DeviceIdType.MESH
DIRS = ((-1, 0), (1, 0), (0, -1), (0, 1), (-1, -1), (-1, 1), (1, -1), (1, 1))
HALO = SWEEPS


def both(a, b):
    return jnp.logical_and(a, b)


def kernel(
    counts,
    direct,
    entries,
    vel_hbm, forc_hbm, visc_hbm, rp_hbm, gp_hbm, hres_hbm, hval_hbm,
    out_ref, res_ref,
    wide, static, hist, late, ahead, past_res, past_val, coef, first, second, fres, delta,
    slots_y, slots_x, slots_all,
    in_sem, send_sem, recv_sem, ysend, yrecv, xsend, xrecv, asend, arecv, gate,
):
    depth, _, cells_x, cells_y, lanes = hres_hbm.shape
    count_x, count_y = counts
    me_x, me_y = lax.axis_index("gx"), lax.axis_index("gy")
    rows = 2 * cells_y

    def exists(sx, sy):
        ok = None
        for step, me, count in ((sx, me_x, count_x), (sy, me_y, count_y)):
            if step != 0:
                here = me > 0 if step < 0 else me < count - 1
                ok = here if ok is None else both(ok, here)
        return ok

    loads = [
        pltpu.make_async_copy(vel_hbm, wide.at[:, HALO : HALO + cells_x, 0:cells_y], in_sem.at[0]),
        pltpu.make_async_copy(forc_hbm, static.at[0:3, 2 : 2 + cells_x, 0:cells_y], in_sem.at[1]),
        pltpu.make_async_copy(visc_hbm, static.at[3, 2 : 2 + cells_x, 0:cells_y], in_sem.at[2]),
        pltpu.make_async_copy(hval_hbm, hist.at[:, :, HALO : HALO + cells_x, 0:cells_y], in_sem.at[3]),
        pltpu.make_async_copy(hres_hbm, fres, in_sem.at[4]),
        pltpu.make_async_copy(rp_hbm, past_res, in_sem.at[5]),
        pltpu.make_async_copy(gp_hbm, past_val, in_sem.at[6]),
    ]
    barrier = pltpu.get_barrier_semaphore()
    for k in range(1, count_y):
        pl.semaphore_signal(
            barrier, inc=1, device_id=(me_x, lax.rem(me_y + k, count_y)), device_id_type=MESH
        )
    for k in range(1, count_x):
        pl.semaphore_signal(
            barrier, inc=1, device_id=(lax.rem(me_x + k, count_x), me_y), device_id_type=MESH
        )
    total = jnp.int32(count_x + count_y - 2)
    for sx, sy in DIRS[4:]:
        here = exists(sx, sy)
        total = total + jnp.where(here, 1, 0)

        @pl.when(here)
        def _():
            pl.semaphore_signal(
                barrier, inc=1, device_id=(me_x + sx, me_y + sy), device_id_type=MESH
            )

    for load in loads:
        load.start()

    def clear(ref, off):
        lead = (slice(None),) * (len(ref.shape) - 3)
        for (sx, sy), part in (
            ((-1, 0), (slice(0, off), slice(None))),
            ((1, 0), (slice(off + cells_x, 2 * off + cells_x), slice(None))),
            ((0, -1), (slice(None), slice(rows - off, rows))),
            ((0, 1), (slice(None), slice(cells_y, cells_y + off))),
        ):

            @pl.when(jnp.logical_not(exists(sx, sy)))
            def _():
                where = lead + part
                ref[where] = jnp.zeros(ref.at[where].shape, jnp.float32)

    clear(wide, HALO)
    clear(static, HALO - 1)
    pl.semaphore_wait(barrier, total)

    def halo(ref, which, d, off):
        sx, sy = DIRS[d]
        wide_by = off if sx == 0 or sy == 0 else off - 1
        if sx == 0:
            src_x = dst_x = slice(off, off + cells_x)
        elif sx < 0:
            src_x = slice(off, off + wide_by)
            dst_x = slice(off + cells_x, off + cells_x + wide_by)
        else:
            src_x = slice(off + cells_x - wide_by, off + cells_x)
            dst_x = slice(off - wide_by, off)
        if sy == 0:
            src_y = dst_y = slice(0, cells_y)
        elif sy < 0:
            src_y = slice(0, wide_by)
            dst_y = slice(cells_y, cells_y + wide_by)
        else:
            src_y = slice(cells_y - wide_by, cells_y)
            dst_y = slice(rows - wide_by, rows)
        lead = (slice(None),) * (len(ref.shape) - 3)
        return pltpu.make_async_remote_copy(
            src_ref=ref.at[lead + (src_x, src_y)],
            dst_ref=ref.at[lead + (dst_x, dst_y)],
            send_sem=send_sem.at[which, d],
            recv_sem=recv_sem.at[which, d],
            device_id=(me_x + sx, me_y + sy),
            device_id_type=MESH,
        )

    fields = ((wide, 0, HALO), (static, 1, HALO - 1), (hist, 2, HALO), (late, 3, HALO))

    def send(field):
        ref, which, off = field
        for d, (sx, sy) in enumerate(DIRS):

            @pl.when(exists(sx, sy))
            def _():
                halo(ref, which, d, off).start()

    def receive(field):
        ref, which, off = field
        for d, (sx, sy) in enumerate(DIRS):

            @pl.when(exists(-sx, -sy))
            def _():
                halo(ref, which, d, off).wait_recv()

    def sent(field):
        ref, which, off = field
        for d, (sx, sy) in enumerate(DIRS):

            @pl.when(exists(sx, sy))
            def _():
                halo(ref, which, d, off).wait_send()

    def along(slots, idx, k, sends, recvs, me, count, axis):
        return pltpu.make_async_remote_copy(
            src_ref=slots.at[idx, me],
            dst_ref=slots.at[idx, me],
            send_sem=sends.at[idx, k],
            recv_sem=recvs.at[idx, k],
            device_id={axis: lax.rem(me + k, count)},
            device_id_type=MESH,
        )

    lines = (
        (slots_y, ysend, yrecv, me_y, count_y, "gy"),
        (slots_x, xsend, xrecv, me_x, count_x, "gx"),
    )

    def spread(line, idx, row):
        slots, sends, recvs, me, count, axis = line
        slots[idx, me] = row
        for k in range(1, count):
            along(slots, idx, k, sends, recvs, me, count, axis).start()

    def gather(line, idx):
        slots, sends, recvs, me, count, axis = line
        for k in range(1, count):
            along(slots, idx, k, sends, recvs, me, count, axis).wait_recv()
        total = slots[idx, 0]
        for k in range(1, count):
            total = total + slots[idx, k]
        return total

    def spent(line, idx):
        slots, sends, recvs, me, count, axis = line
        for k in range(1, count):
            along(slots, idx, k, sends, recvs, me, count, axis).wait_send()

    count_all = count_x * count_y
    me_all = me_x * count_y + me_y

    def straight(k):
        peer = lax.rem(me_all + k, count_all)
        return pltpu.make_async_remote_copy(
            src_ref=slots_all.at[me_all],
            dst_ref=slots_all.at[me_all],
            send_sem=asend.at[k],
            recv_sem=arecv.at[k],
            device_id=(lax.div(peer, count_y), lax.rem(peer, count_y)),
            device_id_type=MESH,
        )

    lane = lax.broadcasted_iota(jnp.int32, (cells_y, lanes), 1)

    def packed(parts):
        row = jnp.zeros((cells_y, lanes), jnp.float32)
        for j, part in enumerate(parts):
            row = jnp.where(lane == j, jnp.sum(part, axis=1, keepdims=True), row)
        return jnp.sum(row, axis=0, keepdims=True)

    def unpacked(row, count):
        return [jnp.broadcast_to(row[:, j : j + 1], (cells_y, lanes)) for j in range(count)]

    own = [(c, x) for c in range(3) for x in range(cells_x)]

    def factored(gram):
        trace = gram[0][0]
        for j in range(1, depth):
            trace = trace + gram[j][j]
        shift = (REG / depth) * trace + FLOOR * entries
        lower = [[None] * depth for _ in range(depth)]
        inverse = [None] * depth
        scaled = [[None] * depth for _ in range(depth)]
        for j in range(depth):
            pivot = gram[j][j] + shift
            for k in range(j):
                pivot = pivot - lower[j][k] * scaled[j][k]
            inverse[j] = 1.0 / pivot
            for i in range(j + 1, depth):
                value = gram[i][j]
                for k in range(j):
                    value = value - scaled[i][k] * lower[j][k]
                scaled[i][j] = value
                lower[i][j] = value * inverse[j]
        return lower, inverse

    def solved(factors, rhs):
        lower, inverse = factors
        part = list(rhs)
        for j in range(depth):
            for i in range(j + 1, depth):
                part[i] = part[i] - lower[i][j] * part[j]
        part = [p * inv for p, inv in zip(part, inverse)]
        for j in reversed(range(depth)):
            for i in range(j):
                part[i] = part[i] - lower[j][i] * part[j]
        return part

    zlane = lax.broadcasted_iota(jnp.int32, (rows, lanes), 1)
    has_below = jnp.where(zlane == 0, 0.0, 1.0)
    has_above = jnp.where(zlane == lanes - 1, 0.0, 1.0)

    def relax(src, dst, off, x, cut):
        cs = [coef[j, x + off][0:cut] for j in range(6)]
        for c in range(3):
            here = src(c, x)
            total = coef[6 + c, x + off][0:cut]
            total = total + cs[0] * src(c, x - 1)[0:cut] + cs[1] * src(c, x + 1)[0:cut]
            total = total + cs[2] * pltpu.roll(here, 1, 0)[0:cut]
            total = total + cs[3] * pltpu.roll(here, rows - 1, 0)[0:cut]
            total = total + cs[4] * pltpu.roll(here[0:cut], 1, 1)
            total = total + cs[5] * pltpu.roll(here[0:cut], lanes - 1, 1)
            dst(c, x, total)

    def picard(field, dst):
        for x in range(-2, cells_x + 2):
            vel = [field[c, x + HALO] for c in range(3)]
            visc = static[3, x + 2]
            diag = 1.0 + 6.0 * visc + jnp.abs(vel[0]) + jnp.abs(vel[1]) + jnp.abs(vel[2])
            inv = 1.0 / diag
            for a in range(3):
                lo = (visc + jnp.maximum(vel[a], 0.0)) * inv
                hi = (visc - jnp.minimum(vel[a], 0.0)) * inv
                if a == 2:
                    lo, hi = lo * has_below, hi * has_above
                coef[2 * a, x + 2] = lo
                coef[2 * a + 1, x + 2] = hi
            for c in range(3):
                coef[6 + c, x + 2] = (static[c, x + 2] + vel[c]) * inv

        def put(ref, off):
            def store(c, x, value):
                ref[c, x + off] = value

            return store

        for x in range(-2, cells_x + 2):
            relax(lambda c, i: field[c, i + HALO], put(first, 2), 2, x, rows)
        for x in range(-1, cells_x + 1):
            relax(lambda c, i: first[c, i + 2], put(second, 1), 2, x, rows)
        for x in range(cells_x):
            relax(lambda c, i: second[c, i + 1], dst, 2, x, cells_y)

    for k in range(1, count_x if direct else 1):
        pl.semaphore_signal(
            gate, inc=1, device_id=(lax.rem(me_x + k, count_x), me_y), device_id_type=MESH
        )

    for load in loads[:3]:
        load.wait()
    send(fields[0])
    send(fields[1])
    loads[3].wait()
    send(fields[2])
    for load in loads[4:]:
        load.wait()

    pairs = [(i, j) for i in range(depth) for j in range(i + 1)]
    clear(hist, HALO)
    clear(late, HALO)
    sums = [None] * (len(pairs) + depth)

    def add(j, value):
        sums[j] = value if sums[j] is None else sums[j] + value

    for c, x in own:
        f = [fres[j, c, x] for j in range(depth)]
        r = past_res[c, x]
        for n, (i, j) in enumerate(pairs):
            add(n, f[i] * f[j])
        for j in range(depth):
            add(len(pairs) + j, f[j] * r)
    spread(lines[1], 0, packed(sums))

    receive(fields[0])
    receive(fields[1])

    def store_value(c, x, value):
        late[c, x + HALO, 0:cells_y] = value

    picard(wide, store_value)

    sums = [None] * (depth + 1)
    for c, x in own:
        resid = late[c, x + HALO, 0:cells_y] - wide[c, x + HALO, 0:cells_y]
        newest = resid - past_res[c, x]
        delta[c, x] = newest
        for j in range(depth):
            add(j, fres[j, c, x] * resid)
        add(depth, newest * newest)
    spread(lines[1], 1, packed(sums))
    send(fields[3])
    spread(lines[0], 0, gather(lines[1], 0))
    spread(lines[0], 1, gather(lines[1], 1))

    early = unpacked(gather(lines[0], 0), len(pairs) + depth)
    gram = [[None] * depth for _ in range(depth)]
    for n, (i, j) in enumerate(pairs):
        gram[i][j] = gram[j][i] = early[n]
    factors = factored(gram)
    receive(fields[2])
    receive(fields[3])
    for_rhs = unpacked(gather(lines[0], 1), depth + 1)
    rhs, newest_sq = for_rhs[:depth], for_rhs[depth]
    gamma = solved(factors, rhs)
    wide_gamma = [jnp.concatenate([g, g], 0) for g in gamma]
    for c in range(3):
        for x in range(cells_x + 2 * HALO):
            value = late[c, x]
            for j in range(depth):
                value = value - wide_gamma[j] * hist[j, c, x]
            ahead[c, x] = value

    def store_out(c, x, value):
        out_ref[c, x] = value

    picard(ahead, store_out)

    sums = [None] * depth
    for c, x in own:
        resid = out_ref[c, x] - ahead[c, x + HALO, 0:cells_y]
        res_ref[c, x] = resid
        for j in range(1, depth):
            add(j - 1, fres[j, c, x] * resid)
        add(depth - 1, delta[c, x] * resid)
    if direct:
        pl.semaphore_wait(gate, count_x - 1)
        slots_all[me_all] = packed(sums)
        for k in range(1, count_all):
            straight(k).start()
    else:
        spread(lines[1], 2, packed(sums))

    gram2 = [[None] * depth for _ in range(depth)]
    for i in range(depth - 1):
        for j in range(depth - 1):
            gram2[i][j] = gram[i + 1][j + 1]
        cross = rhs[i + 1] - early[len(pairs) + i + 1]
        gram2[i][depth - 1] = gram2[depth - 1][i] = cross
    gram2[depth - 1][depth - 1] = newest_sq
    factors = factored(gram2)

    if not direct:
        spread(lines[0], 2, gather(lines[1], 2))
    for field in fields:
        sent(field)
    for line in lines:
        for idx in range(2):
            spent(line, idx)
    if direct:
        for k in range(1, count_all):
            straight(k).wait_recv()
        final = jnp.sum(slots_all[...], axis=0)
    else:
        final = gather(lines[0], 2)
    gamma = solved(factors, unpacked(final, depth))
    for c, x in own:
        value = out_ref[c, x]
        newest = late[c, x + HALO, 0:cells_y] - past_val[c, x]
        for j in range(1, depth):
            value = value - gamma[j - 1] * hist[j, c, x + HALO, 0:cells_y]
        out_ref[c, x] = value - gamma[depth - 1] * newest
    if direct:
        for k in range(1, count_all):
            straight(k).wait_send()
    else:
        for line in lines:
            spent(line, 2)


def leave(vel_ref, res_ref, vel_hbm, res_hbm, sem):
    copies = [
        pltpu.make_async_copy(vel_ref, vel_hbm, sem.at[0]),
        pltpu.make_async_copy(res_ref, res_hbm, sem.at[1]),
    ]
    for copy in copies:
        copy.start()
    for copy in copies:
        copy.wait()


def local(velocity, forcing, viscosity, residual_prev, value_prev, hist_res, hist_val):
    depth, comps, cells_x, cells_y, lanes = hist_res.shape
    counts = (lax.axis_size("gx"), lax.axis_size("gy"))
    entries = 3.0 * cells_x * cells_y * lanes * counts[0] * counts[1]
    rows = 2 * cells_y
    count_all = counts[0] * counts[1]
    direct = count_all <= 64
    count_all = count_all if direct else 1

    def vmem(*shape):
        return pltpu.VMEM(shape + (lanes,), jnp.float32)

    results = pl.pallas_call(
        functools.partial(kernel, counts, direct, entries),
        name="anderson",
        out_shape=(pltpu.VMEM(velocity.shape, jnp.float32),) * 2,
        in_specs=[pl.BlockSpec(memory_space=pl.ANY)] * 7,
        out_specs=(pl.BlockSpec(memory_space=pltpu.VMEM),) * 2,
        scratch_shapes=[
            vmem(3, cells_x + 6, rows),
            vmem(4, cells_x + 4, rows),
            vmem(depth, 3, cells_x + 6, rows),
            vmem(3, cells_x + 6, rows),
            vmem(3, cells_x + 6, rows),
            vmem(3, cells_x, cells_y),
            vmem(3, cells_x, cells_y),
            vmem(9, cells_x + 4, rows),
            vmem(3, cells_x + 4, rows),
            vmem(3, cells_x + 2, rows),
            vmem(depth, 3, cells_x, cells_y),
            vmem(3, cells_x, cells_y),
            vmem(3, counts[1], 1),
            vmem(3, counts[0], 1),
            vmem(count_all, 1),
            pltpu.SemaphoreType.DMA((7,)),
            pltpu.SemaphoreType.DMA((4, 8)),
            pltpu.SemaphoreType.DMA((4, 8)),
            pltpu.SemaphoreType.DMA((3, counts[1])),
            pltpu.SemaphoreType.DMA((3, counts[1])),
            pltpu.SemaphoreType.DMA((3, counts[0])),
            pltpu.SemaphoreType.DMA((3, counts[0])),
            pltpu.SemaphoreType.DMA((count_all,)),
            pltpu.SemaphoreType.DMA((count_all,)),
            pltpu.SemaphoreType.REGULAR,
        ],
        compiler_params=pltpu.CompilerParams(collective_id=0, has_side_effects=True),
    )(velocity, forcing, viscosity, residual_prev, value_prev, hist_res, hist_val)
    return pl.pallas_call(
        leave,
        name="leave",
        out_shape=(jax.ShapeDtypeStruct(velocity.shape, jnp.float32),) * 2,
        in_specs=[pl.BlockSpec(memory_space=pl.ANY)] * 2,
        out_specs=(pl.BlockSpec(memory_space=pl.ANY),) * 2,
        scratch_shapes=[pltpu.SemaphoreType.DMA((2,))],
    )(*(pltpu.with_memory_space_constraint(r, pltpu.VMEM) for r in results))


def solution(mesh):
    field = P(None, "gx", "gy", None)
    history = P(None, None, "gx", "gy", None)
    return jax.shard_map(
        local,
        mesh=mesh,
        in_specs=(field, field, P("gx", "gy", None), field, field, history, history),
        out_specs=(field, field),
        check_vma=False,
    )
```

profile of v0, /device:TPU:0, one launch (start us, length us, event | category | flops | bytes accessed | tf_op | source)
XLA Modules:
  0.0 25.4 jit_solution(9386771209225901678)
XLA Ops:
  0.6 24.1 %anderson.1 = (f32[3,4,8,128]{3,2,1,0:T(8,128)S(1)}, f32[3,4,8,128]{3,2,1,0:T(8,128)S(1)}) custom-call(f32[3,4,8,128]{3,2,1,0:T(8,128)} %vel_hbm.1, f32[3,4,8,128]{3,2,1,0:T(8,128)} %forc_hbm.1, f32[4,8,128]{2,1,0:T(8,128)} %visc_hbm.1, f32[3,4,8,128]{3,2,1,0:T(8,128)} %rp_hbm.1, f32[3,4,8,128]{3,2,1,0:T(8,128)} %gp_hbm.1, f32[5,3,4,8,128]{4,3,2,1,0:T(8,128)} %hres_hbm.1, ...), custom_call_target="tpu_custom_call" | custom-call | tf_op jit(solution)/shard_map/anderson/pallas_call | solution.py:440
  24.8 0.7 %leave.1 = (f32[3,4,8,128]{3,2,1,0:T(8,128)}, f32[3,4,8,128]{3,2,1,0:T(8,128)}) custom-call(f32[3,4,8,128]{3,2,1,0:T(8,128)S(1)} %get-tuple-element.4.vel_ref, f32[3,4,8,128]{3,2,1,0:T(8,128)S(1)} %get-tuple-element.5.res_ref), custom_call_target="tpu_custom_call" | custom-call | tf_op jit(solution)/shard_map/leave/pallas_call | solution.py:475
where the time goes:
time: 25.6 us; the launch traced here: 25.4 us
  Pallas kernels  24.8 us (97%)
  between operations  0.64 us (2%)
    pallas_call x1, Pallas kernels, local(): pl.pallas_call(functools.partial(kernel, counts, direct, entries), name='...  24.1 us
    pallas_call x1, Pallas kernels, local(): pl.pallas_call(leave, name='leave', out_shape=(jax.ShapeDtypeStruct(veloc...  0.66 us

commit v1 on v0

--- a/solution.py
+++ b/solution.py
@@ -26,7 +26,7 @@
     vel_hbm, forc_hbm, visc_hbm, rp_hbm, gp_hbm, hres_hbm, hval_hbm,
     out_ref, res_ref,
     wide, static, hist, late, ahead, past_res, past_val, coef, first, second, fres, delta,
-    slots_y, slots_x, slots_all,
+    slots_y, slots_x, slots_all, ruler,
     in_sem, send_sem, recv_sem, ysend, yrecv, xsend, xrecv, asend, arecv, gate,
 ):
     depth, _, cells_x, cells_y, lanes = hres_hbm.shape
@@ -115,8 +115,8 @@
         return pltpu.make_async_remote_copy(
             src_ref=ref.at[lead + (src_x, src_y)],
             dst_ref=ref.at[lead + (dst_x, dst_y)],
-            send_sem=send_sem.at[which, d],
-            recv_sem=recv_sem.at[which, d],
+            send_sem=send_sem.at[which],
+            recv_sem=recv_sem.at[which],
             device_id=(me_x + sx, me_y + sy),
             device_id_type=MESH,
         )
@@ -131,28 +131,56 @@
             def _():
                 halo(ref, which, d, off).start()
 
+    def places(me, count):
+        inner = both(me > 0, me < count - 1)
+        if count == 1:
+            return [((0, 0), None)]
+        ends = [((0, 1), me == 0), ((1, 0), me == count - 1)]
+        return ends + [((1, 1), inner)] if count > 2 else ends
+
+    def moved(field, act):
+        ref, which, off = field
+        lead = 1
+        for extent in ref.shape[:-3]:
+            lead = lead * extent
+        for sides_x, here_x in places(me_x, count_x):
+            for sides_y, here_y in places(me_y, count_y):
+                size = 0
+                for sx, sy in DIRS:
+                    deep = off if sx == 0 or sy == 0 else off - 1
+                    part = lead * (cells_x if sx == 0 else deep) * (cells_y if sy == 0 else deep)
+                    for step, sides in ((sx, sides_x), (sy, sides_y)):
+                        part = part * (sides[(step + 1) // 2] if step != 0 else 1)
+                    size = size + part
+                if size == 0:
+                    continue
+                rows_all = ruler.at[0:size]
+                copy = pltpu.make_async_remote_copy(
+                    src_ref=rows_all,
+                    dst_ref=rows_all,
+                    send_sem=send_sem.at[which],
+                    recv_sem=recv_sem.at[which],
+                    device_id={"gx": lax.rem(me_x + 1, count_x)},
+                    device_id_type=MESH,
+                )
+                here = [h for h in (here_x, here_y) if h is not None]
+
+                @pl.when(functools.reduce(both, here))
+                def _():
+                    act(copy)
+
     def receive(field):
-        ref, which, off = field
-        for d, (sx, sy) in enumerate(DIRS):
-
-            @pl.when(exists(-sx, -sy))
-            def _():
-                halo(ref, which, d, off).wait_recv()
+        moved(field, lambda copy: copy.wait_recv())
 
     def sent(field):
-        ref, which, off = field
-        for d, (sx, sy) in enumerate(DIRS):
-
-            @pl.when(exists(sx, sy))
-            def _():
-                halo(ref, which, d, off).wait_send()
+        moved(field, lambda copy: copy.wait_send())
 
     def along(slots, idx, k, sends, recvs, me, count, axis):
         return pltpu.make_async_remote_copy(
             src_ref=slots.at[idx, me],
             dst_ref=slots.at[idx, me],
-            send_sem=sends.at[idx, k],
-            recv_sem=recvs.at[idx, k],
+            send_sem=sends.at[idx],
+            recv_sem=recvs.at[idx],
             device_id={axis: lax.rem(me + k, count)},
             device_id_type=MESH,
         )
@@ -168,19 +196,28 @@
         for k in range(1, count):
             along(slots, idx, k, sends, recvs, me, count, axis).start()
 
+    def whole(line, idx):
+        slots, sends, recvs, me, count, axis = line
+        part = slots.at[idx, 0 : count - 1]
+        return pltpu.make_async_remote_copy(
+            src_ref=part,
+            dst_ref=part,
+            send_sem=sends.at[idx],
+            recv_sem=recvs.at[idx],
+            device_id={axis: lax.rem(me + 1, count)},
+            device_id_type=MESH,
+        )
+
     def gather(line, idx):
         slots, sends, recvs, me, count, axis = line
-        for k in range(1, count):
-            along(slots, idx, k, sends, recvs, me, count, axis).wait_recv()
+        whole(line, idx).wait_recv()
         total = slots[idx, 0]
         for k in range(1, count):
             total = total + slots[idx, k]
         return total
 
     def spent(line, idx):
-        slots, sends, recvs, me, count, axis = line
-        for k in range(1, count):
-            along(slots, idx, k, sends, recvs, me, count, axis).wait_send()
+        whole(line, idx).wait_send()
 
     count_all = count_x * count_y
     me_all = me_x * count_y + me_y
@@ -190,9 +227,20 @@
         return pltpu.make_async_remote_copy(
             src_ref=slots_all.at[me_all],
             dst_ref=slots_all.at[me_all],
-            send_sem=asend.at[k],
-            recv_sem=arecv.at[k],
+            send_sem=asend,
+            recv_sem=arecv,
             device_id=(lax.div(peer, count_y), lax.rem(peer, count_y)),
+            device_id_type=MESH,
+        )
+
+    def all_straight():
+        part = slots_all.at[0 : count_all - 1]
+        return pltpu.make_async_remote_copy(
+            src_ref=part,
+            dst_ref=part,
+            send_sem=asend,
+            recv_sem=arecv,
+            device_id={"gx": lax.rem(me_x + 1, count_x)},
             device_id_type=MESH,
         )
 
@@ -394,8 +442,7 @@
         for idx in range(2):
             spent(line, idx)
     if direct:
-        for k in range(1, count_all):
-            straight(k).wait_recv()
+        all_straight().wait_recv()
         final = jnp.sum(slots_all[...], axis=0)
     else:
         final = gather(lines[0], 2)
@@ -407,8 +454,7 @@
             value = value - gamma[j - 1] * hist[j, c, x + HALO, 0:cells_y]
         out_ref[c, x] = value - gamma[depth - 1] * newest
     if direct:
-        for k in range(1, count_all):
-            straight(k).wait_send()
+        all_straight().wait_send()
     else:
         for line in lines:
             spent(line, 2)
@@ -459,15 +505,16 @@
             vmem(3, counts[1], 1),
             vmem(3, counts[0], 1),
             vmem(count_all, 1),
+            vmem(depth * 3 * (6 * (cells_x + cells_y) + 16), 1),
             pltpu.SemaphoreType.DMA((7,)),
-            pltpu.SemaphoreType.DMA((4, 8)),
-            pltpu.SemaphoreType.DMA((4, 8)),
-            pltpu.SemaphoreType.DMA((3, counts[1])),
-            pltpu.SemaphoreType.DMA((3, counts[1])),
-            pltpu.SemaphoreType.DMA((3, counts[0])),
-            pltpu.SemaphoreType.DMA((3, counts[0])),
-            pltpu.SemaphoreType.DMA((count_all,)),
-            pltpu.SemaphoreType.DMA((count_all,)),
+            pltpu.SemaphoreType.DMA((4,)),
+            pltpu.SemaphoreType.DMA((4,)),
+            pltpu.SemaphoreType.DMA((3,)),
+            pltpu.SemaphoreType.DMA((3,)),
+            pltpu.SemaphoreType.DMA((3,)),
+            pltpu.SemaphoreType.DMA((3,)),
+            pltpu.SemaphoreType.DMA,
+            pltpu.SemaphoreType.DMA,
             pltpu.SemaphoreType.REGULAR,
         ],
         compiler_params=pltpu.CompilerParams(collective_id=0, has_side_effects=True),

time: 25.6 us -> 23.9 us (0.934)
  Pallas kernels: 24.8 us -> 23.1 us
    pallas_call x1, Pallas kernels: 24.1 us -> 22.5 us  [local(): pl.pallas_call(functools.partial(kernel, counts, direct, entries), name='...]
where the time goes in v1:
time: 23.9 us; the launch traced here: 23.8 us
  Pallas kernels  23.1 us (97%)
  between operations  0.64 us (3%)
    pallas_call x1, Pallas kernels, local(): pl.pallas_call(functools.partial(kernel, counts, direct, entries), name='...  22.5 us
    pallas_call x1, Pallas kernels, local(): pl.pallas_call(leave, name='leave', out_shape=(jax.ShapeDtypeStruct(veloc...  0.66 us

profile of v1, /device:TPU:0, one launch (start us, length us, event | category | flops | bytes accessed | tf_op | source)
XLA Modules:
  0.0 23.8 jit_solution(6380879585984126827)
XLA Ops:
  0.6 22.5 %anderson.1 = (f32[3,4,8,128]{3,2,1,0:T(8,128)S(1)}, f32[3,4,8,128]{3,2,1,0:T(8,128)S(1)}) custom-call(f32[3,4,8,128]{3,2,1,0:T(8,128)} %vel_hbm.1, f32[3,4,8,128]{3,2,1,0:T(8,128)} %forc_hbm.1, f32[4,8,128]{2,1,0:T(8,128)} %visc_hbm.1, f32[3,4,8,128]{3,2,1,0:T(8,128)} %rp_hbm.1, f32[3,4,8,128]{3,2,1,0:T(8,128)} %gp_hbm.1, f32[5,3,4,8,128]{4,3,2,1,0:T(8,128)} %hres_hbm.1, ...), custom_call_target="tpu_custom_call" | custom-call | tf_op jit(solution)/shard_map/anderson/pallas_call | solution.py:486
  23.1 0.7 %leave.1 = (f32[3,4,8,128]{3,2,1,0:T(8,128)}, f32[3,4,8,128]{3,2,1,0:T(8,128)}) custom-call(f32[3,4,8,128]{3,2,1,0:T(8,128)S(1)} %get-tuple-element.4.vel_ref, f32[3,4,8,128]{3,2,1,0:T(8,128)S(1)} %get-tuple-element.5.res_ref), custom_call_target="tpu_custom_call" | custom-call | tf_op jit(solution)/shard_map/leave/pallas_call | solution.py:522

commit v2 on v1

--- a/solution.py
+++ b/solution.py
@@ -26,8 +26,7 @@
     vel_hbm, forc_hbm, visc_hbm, rp_hbm, gp_hbm, hres_hbm, hval_hbm,
     out_ref, res_ref,
     wide, static, hist, late, ahead, past_res, past_val, coef, first, second, fres, delta,
-    slots_y, slots_x, slots_all, ruler,
-    in_sem, send_sem, recv_sem, ysend, yrecv, xsend, xrecv, asend, arecv, gate,
+    ruler, in_sem, send_sem, recv_sem, gate, *shared,
 ):
     depth, _, cells_x, cells_y, lanes = hres_hbm.shape
     count_x, count_y = counts
@@ -51,6 +50,8 @@
         pltpu.make_async_copy(rp_hbm, past_res, in_sem.at[5]),
         pltpu.make_async_copy(gp_hbm, past_val, in_sem.at[6]),
     ]
+    for load in loads:
+        load.start()
     barrier = pltpu.get_barrier_semaphore()
     for k in range(1, count_y):
         pl.semaphore_signal(
@@ -71,9 +72,6 @@
                 barrier, inc=1, device_id=(me_x + sx, me_y + sy), device_id_type=MESH
             )
 
-    for load in loads:
-        load.start()
-
     def clear(ref, off):
         lead = (slice(None),) * (len(ref.shape) - 3)
         for (sx, sy), part in (
@@ -90,76 +88,78 @@
 
     clear(wide, HALO)
     clear(static, HALO - 1)
-    pl.semaphore_wait(barrier, total)
-
-    def halo(ref, which, d, off):
-        sx, sy = DIRS[d]
-        wide_by = off if sx == 0 or sy == 0 else off - 1
+    with jax.named_scope("barrier"):
+        pl.semaphore_wait(barrier, total)
+
+    def span_x(sx, off, deep, skip=0):
         if sx == 0:
-            src_x = dst_x = slice(off, off + cells_x)
-        elif sx < 0:
-            src_x = slice(off, off + wide_by)
-            dst_x = slice(off + cells_x, off + cells_x + wide_by)
-        else:
-            src_x = slice(off + cells_x - wide_by, off + cells_x)
-            dst_x = slice(off - wide_by, off)
+            return (slice(off, off + cells_x),) * 2
+        if sx < 0:
+            return slice(off + skip, off + deep), slice(off + cells_x + skip, off + cells_x + deep)
+        return slice(off + cells_x - deep, off + cells_x - skip), slice(off - deep, off - skip)
+
+    def span_y(sy, deep, skip=0):
         if sy == 0:
-            src_y = dst_y = slice(0, cells_y)
-        elif sy < 0:
-            src_y = slice(0, wide_by)
-            dst_y = slice(cells_y, cells_y + wide_by)
-        else:
-            src_y = slice(cells_y - wide_by, cells_y)
-            dst_y = slice(rows - wide_by, rows)
-        lead = (slice(None),) * (len(ref.shape) - 3)
-        return pltpu.make_async_remote_copy(
-            src_ref=ref.at[lead + (src_x, src_y)],
-            dst_ref=ref.at[lead + (dst_x, dst_y)],
-            send_sem=send_sem.at[which],
-            recv_sem=recv_sem.at[which],
-            device_id=(me_x + sx, me_y + sy),
-            device_id_type=MESH,
-        )
-
-    fields = ((wide, 0, HALO), (static, 1, HALO - 1), (hist, 2, HALO), (late, 3, HALO))
-
-    def send(field):
-        ref, which, off = field
-        for d, (sx, sy) in enumerate(DIRS):
-
-            @pl.when(exists(sx, sy))
-            def _():
-                halo(ref, which, d, off).start()
+            return (slice(0, cells_y),) * 2
+        if sy < 0:
+            return slice(skip, deep), slice(cells_y + skip, cells_y + deep)
+        return slice(cells_y - deep, cells_y - skip), slice(rows - deep, rows - skip)
+
+    def faces(ref, off, dirs):
+        pieces = []
+        for sx, sy in dirs:
+            deep = off if sx == 0 or sy == 0 else off - 1
+            pieces.append((ref, (sx, sy), 0, span_x(sx, off, deep), span_y(sy, deep)))
+        return pieces
+
+    def layers(ref, off, deep, skip):
+        return [(ref, (0, sy), 0, span_x(0, off, 0), span_y(sy, deep, skip)) for sy in (-1, 1)]
+
+    def corners(ref, off):
+        deep = off - 1
+        pieces = []
+        for sx in (-1, 1):
+            for side, part in ((1, slice(cells_y, cells_y + deep)), (-1, slice(rows - deep, rows))):
+                pieces.append((ref, (sx, 0), side, span_x(sx, off, deep), (part, part)))
+        return pieces
+
+    def length(part):
+        return part.stop - part.start
+
+    def size_of(piece):
+        ref, _, _, (src_x, _), (src_y, _) = piece
+        size = length(src_x) * length(src_y)
+        for extent in ref.shape[:-3]:
+            size = size * extent
+        return size
 
     def places(me, count):
-        inner = both(me > 0, me < count - 1)
         if count == 1:
             return [((0, 0), None)]
         ends = [((0, 1), me == 0), ((1, 0), me == count - 1)]
-        return ends + [((1, 1), inner)] if count > 2 else ends
-
-    def moved(field, act):
-        ref, which, off = field
-        lead = 1
-        for extent in ref.shape[:-3]:
-            lead = lead * extent
+        return ends + [((1, 1), both(me > 0, me < count - 1))] if count > 2 else ends
+
+    def settle(pieces, sem, sending, more=0):
         for sides_x, here_x in places(me_x, count_x):
             for sides_y, here_y in places(me_y, count_y):
-                size = 0
-                for sx, sy in DIRS:
-                    deep = off if sx == 0 or sy == 0 else off - 1
-                    part = lead * (cells_x if sx == 0 else deep) * (cells_y if sy == 0 else deep)
+                size = more
+                for piece in pieces:
+                    _, (sx, sy), side, _, _ = piece
+                    there = 1
                     for step, sides in ((sx, sides_x), (sy, sides_y)):
-                        part = part * (sides[(step + 1) // 2] if step != 0 else 1)
-                    size = size + part
+                        if step != 0:
+                            there = there * sides[step > 0 if sending else step < 0]
+                    if side != 0:
+                        there = there * sides_y[side > 0]
+                    size = size + there * size_of(piece)
                 if size == 0:
                     continue
-                rows_all = ruler.at[0:size]
+                part = ruler.at[0:size]
                 copy = pltpu.make_async_remote_copy(
-                    src_ref=rows_all,
-                    dst_ref=rows_all,
-                    send_sem=send_sem.at[which],
-                    recv_sem=recv_sem.at[which],
+                    src_ref=part,
+                    dst_ref=part,
+                    send_sem=sem,
+                    recv_sem=sem,
                     device_id={"gx": lax.rem(me_x + 1, count_x)},
                     device_id_type=MESH,
                 )
@@ -167,13 +167,44 @@
 
                 @pl.when(functools.reduce(both, here))
                 def _():
-                    act(copy)
-
-    def receive(field):
-        moved(field, lambda copy: copy.wait_recv())
-
-    def sent(field):
-        moved(field, lambda copy: copy.wait_send())
+                    if sending:
+                        copy.wait_send()
+                    else:
+                        copy.wait_recv()
+
+    fields = {
+        "wide": faces(wide, HALO, DIRS),
+        "static": faces(static, HALO - 1, DIRS),
+        "across": faces(hist, HALO, DIRS[:2]),
+        "near": layers(hist, HALO, HALO - 1, 0),
+        "far": layers(hist, HALO, HALO, HALO - 1),
+        "turn": corners(hist, HALO),
+        "late": faces(late, HALO, DIRS),
+    }
+    places_of = {name: n for n, name in enumerate(fields)}
+
+    def send(name):
+        for piece in fields[name]:
+            ref, (sx, sy), side, (src_x, dst_x), (src_y, dst_y) = piece
+            here = exists(sx, sy)
+            if side != 0:
+                here = both(here, exists(0, side))
+            lead = (slice(None),) * (len(ref.shape) - 3)
+
+            @pl.when(here)
+            def _():
+                pltpu.make_async_remote_copy(
+                    src_ref=ref.at[lead + (src_x, src_y)],
+                    dst_ref=ref.at[lead + (dst_x, dst_y)],
+                    send_sem=send_sem,
+                    recv_sem=recv_sem.at[places_of[name]],
+                    device_id=(me_x + sx, me_y + sy),
+                    device_id_type=MESH,
+                ).start()
+
+    def receive(name):
+        with jax.named_scope(name):
+            settle(fields[name], recv_sem.at[places_of[name]], False)
 
     def along(slots, idx, k, sends, recvs, me, count, axis):
         return pltpu.make_async_remote_copy(
@@ -185,10 +216,16 @@
             device_id_type=MESH,
         )
 
-    lines = (
-        (slots_y, ysend, yrecv, me_y, count_y, "gy"),
-        (slots_x, xsend, xrecv, me_x, count_x, "gx"),
-    )
+    count_all = count_x * count_y
+    me_all = me_x * count_y + me_y
+    if direct:
+        slots_all, all_sem = shared
+    else:
+        slots_y, slots_x, ysend, yrecv, xsend, xrecv = shared
+        lines = (
+            (slots_y, ysend, yrecv, me_y, count_y, "gy"),
+            (slots_x, xsend, xrecv, me_x, count_x, "gx"),
+        )
 
     def spread(line, idx, row):
         slots, sends, recvs, me, count, axis = line
@@ -216,33 +253,40 @@
             total = total + slots[idx, k]
         return total
 
-    def spent(line, idx):
-        whole(line, idx).wait_send()
-
-    count_all = count_x * count_y
-    me_all = me_x * count_y + me_y
-
-    def straight(k):
-        peer = lax.rem(me_all + k, count_all)
-        return pltpu.make_async_remote_copy(
-            src_ref=slots_all.at[me_all],
-            dst_ref=slots_all.at[me_all],
-            send_sem=asend,
-            recv_sem=arecv,
-            device_id=(lax.div(peer, count_y), lax.rem(peer, count_y)),
-            device_id_type=MESH,
-        )
-
-    def all_straight():
-        part = slots_all.at[0 : count_all - 1]
-        return pltpu.make_async_remote_copy(
-            src_ref=part,
-            dst_ref=part,
-            send_sem=asend,
-            recv_sem=arecv,
-            device_id={"gx": lax.rem(me_x + 1, count_x)},
-            device_id_type=MESH,
-        )
+    def give(idx, row):
+        if not direct:
+            spread(lines[1], idx, row)
+            return
+        slots_all[idx, me_all] = row
+        for k in range(1, count_all):
+            peer = lax.rem(me_all + k, count_all)
+            pltpu.make_async_remote_copy(
+                src_ref=slots_all.at[idx, me_all],
+                dst_ref=slots_all.at[idx, me_all],
+                send_sem=send_sem,
+                recv_sem=all_sem.at[idx],
+                device_id=(lax.div(peer, count_y), lax.rem(peer, count_y)),
+                device_id_type=MESH,
+            ).start()
+
+    def halfway(idx):
+        if not direct:
+            spread(lines[0], idx, gather(lines[1], idx))
+
+    def take(idx):
+        if not direct:
+            return gather(lines[0], idx)
+        part = ruler.at[0 : count_all - 1]
+        with jax.named_scope("take" + str(idx)):
+            pltpu.make_async_remote_copy(
+                src_ref=part,
+                dst_ref=part,
+                send_sem=all_sem.at[idx],
+                recv_sem=all_sem.at[idx],
+                device_id={"gx": lax.rem(me_x + 1, count_x)},
+                device_id_type=MESH,
+            ).wait_recv()
+        return jnp.sum(slots_all[idx], axis=0)
 
     lane = lax.broadcasted_iota(jnp.int32, (cells_y, lanes), 1)
 
@@ -342,10 +386,12 @@
 
     for load in loads[:3]:
         load.wait()
-    send(fields[0])
-    send(fields[1])
+    send("wide")
+    send("static")
     loads[3].wait()
-    send(fields[2])
+    send("near")
+    send("far")
+    send("across")
     for load in loads[4:]:
         load.wait()
 
@@ -364,10 +410,14 @@
             add(n, f[i] * f[j])
         for j in range(depth):
             add(len(pairs) + j, f[j] * r)
-    spread(lines[1], 0, packed(sums))
-
-    receive(fields[0])
-    receive(fields[1])
+    row = packed(sums)
+    if direct:
+        with jax.named_scope("gate"):
+            pl.semaphore_wait(gate, count_x - 1)
+    give(0, row)
+
+    receive("wide")
+    receive("static")
 
     def store_value(c, x, value):
         late[c, x + HALO, 0:cells_y] = value
@@ -382,19 +432,21 @@
         for j in range(depth):
             add(j, fres[j, c, x] * resid)
         add(depth, newest * newest)
-    spread(lines[1], 1, packed(sums))
-    send(fields[3])
-    spread(lines[0], 0, gather(lines[1], 0))
-    spread(lines[0], 1, gather(lines[1], 1))
-
-    early = unpacked(gather(lines[0], 0), len(pairs) + depth)
+    give(1, packed(sums))
+    send("late")
+    receive("near")
+    send("turn")
+    halfway(0)
+    halfway(1)
+
+    early = unpacked(take(0), len(pairs) + depth)
     gram = [[None] * depth for _ in range(depth)]
     for n, (i, j) in enumerate(pairs):
         gram[i][j] = gram[j][i] = early[n]
     factors = factored(gram)
-    receive(fields[2])
-    receive(fields[3])
-    for_rhs = unpacked(gather(lines[0], 1), depth + 1)
+    for name in ("across", "far", "turn", "late"):
+        receive(name)
+    for_rhs = unpacked(take(1), depth + 1)
     rhs, newest_sq = for_rhs[:depth], for_rhs[depth]
     gamma = solved(factors, rhs)
     wide_gamma = [jnp.concatenate([g, g], 0) for g in gamma]
@@ -417,13 +469,7 @@
         for j in range(1, depth):
             add(j - 1, fres[j, c, x] * resid)
         add(depth - 1, delta[c, x] * resid)
-    if direct:
-        pl.semaphore_wait(gate, count_x - 1)
-        slots_all[me_all] = packed(sums)
-        for k in range(1, count_all):
-            straight(k).start()
-    else:
-        spread(lines[1], 2, packed(sums))
+    give(2, packed(sums))
 
     gram2 = [[None] * depth for _ in range(depth)]
     for i in range(depth - 1):
@@ -434,18 +480,8 @@
     gram2[depth - 1][depth - 1] = newest_sq
     factors = factored(gram2)
 
-    if not direct:
-        spread(lines[0], 2, gather(lines[1], 2))
-    for field in fields:
-        sent(field)
-    for line in lines:
-        for idx in range(2):
-            spent(line, idx)
-    if direct:
-        all_straight().wait_recv()
-        final = jnp.sum(slots_all[...], axis=0)
-    else:
-        final = gather(lines[0], 2)
+    halfway(2)
+    final = take(2)
     gamma = solved(factors, unpacked(final, depth))
     for c, x in own:
         value = out_ref[c, x]
@@ -453,11 +489,12 @@
         for j in range(1, depth):
             value = value - gamma[j - 1] * hist[j, c, x + HALO, 0:cells_y]
         out_ref[c, x] = value - gamma[depth - 1] * newest
-    if direct:
-        all_straight().wait_send()
-    else:
+    pieces = [piece for name in fields for piece in fields[name]]
+    settle(pieces, send_sem, True, 3 * (count_all - 1) if direct else 0)
+    if not direct:
         for line in lines:
-            spent(line, 2)
+            for idx in range(3):
+                whole(line, idx).wait_send()
 
 
 def leave(vel_ref, res_ref, vel_hbm, res_hbm, sem):
@@ -478,11 +515,15 @@
     rows = 2 * cells_y
     count_all = counts[0] * counts[1]
     direct = count_all <= 64
-    count_all = count_all if direct else 1
-
     def vmem(*shape):
         return pltpu.VMEM(shape + (lanes,), jnp.float32)
 
+    if direct:
+        shared = [vmem(3, count_all, 1), pltpu.SemaphoreType.DMA((3,))]
+    else:
+        shared = [vmem(3, counts[1], 1), vmem(3, counts[0], 1)]
+        shared += [pltpu.SemaphoreType.DMA((3,))] * 4
+    length = 9 * (depth + 3) * (6 * (cells_x + cells_y) + 16) + 3 * count_all
     results = pl.pallas_call(
         functools.partial(kernel, counts, direct, entries),
         name="anderson",
@@ -502,20 +543,12 @@
             vmem(3, cells_x + 2, rows),
             vmem(depth, 3, cells_x, cells_y),
             vmem(3, cells_x, cells_y),
-            vmem(3, counts[1], 1),
-            vmem(3, counts[0], 1),
-            vmem(count_all, 1),
-            vmem(depth * 3 * (6 * (cells_x + cells_y) + 16), 1),
+            vmem(length, 1),
             pltpu.SemaphoreType.DMA((7,)),
-            pltpu.SemaphoreType.DMA((4,)),
-            pltpu.SemaphoreType.DMA((4,)),
-            pltpu.SemaphoreType.DMA((3,)),
-            pltpu.SemaphoreType.DMA((3,)),
-            pltpu.SemaphoreType.DMA((3,)),
-            pltpu.SemaphoreType.DMA((3,)),
             pltpu.SemaphoreType.DMA,
-            pltpu.SemaphoreType.DMA,
+            pltpu.SemaphoreType.DMA((7,)),
             pltpu.SemaphoreType.REGULAR,
+            *shared,
         ],
         compiler_params=pltpu.CompilerParams(collective_id=0, has_side_effects=True),
     )(velocity, forcing, viscosity, residual_prev, value_prev, hist_res, hist_val)

time: 23.9 us -> 22.1 us (0.925)
  Pallas kernels: 23.1 us -> 21.3 us
    pallas_call x1, Pallas kernels: 22.5 us -> 20.7 us  [local(): pl.pallas_call(functools.partial(kernel, counts, direct, entries), name='...]
where the time goes in v2:
time: 22.1 us; the launch traced here: 22 us
  Pallas kernels  21.3 us (96%)
  between operations  0.64 us (3%)
    pallas_call x1, Pallas kernels, local(): pl.pallas_call(functools.partial(kernel, counts, direct, entries), name='...  20.7 us
    pallas_call x1, Pallas kernels, local(): pl.pallas_call(leave, name='leave', out_shape=(jax.ShapeDtypeStruct(veloc...  0.66 us

profile of v2, /device:TPU:0, one launch (start us, length us, event | category | flops | bytes accessed | tf_op | source)
XLA Modules:
  0.0 22.0 jit_solution(12445929821571989348)
XLA Ops:
  0.6 20.7 %anderson.1 = (f32[3,4,8,128]{3,2,1,0:T(8,128)S(1)}, f32[3,4,8,128]{3,2,1,0:T(8,128)S(1)}) custom-call(f32[3,4,8,128]{3,2,1,0:T(8,128)} %vel_hbm.1, f32[3,4,8,128]{3,2,1,0:T(8,128)} %forc_hbm.1, f32[4,8,128]{2,1,0:T(8,128)} %visc_hbm.1, f32[3,4,8,128]{3,2,1,0:T(8,128)} %rp_hbm.1, f32[3,4,8,128]{3,2,1,0:T(8,128)} %gp_hbm.1, f32[5,3,4,8,128]{4,3,2,1,0:T(8,128)} %hres_hbm.1, ...), custom_call_target="tpu_custom_call" | custom-call | tf_op jit(solution)/shard_map/anderson/pallas_call | solution.py:527
  21.3 0.7 %leave.1 = (f32[3,4,8,128]{3,2,1,0:T(8,128)}, f32[3,4,8,128]{3,2,1,0:T(8,128)}) custom-call(f32[3,4,8,128]{3,2,1,0:T(8,128)S(1)} %get-tuple-element.4.vel_ref, f32[3,4,8,128]{3,2,1,0:T(8,128)S(1)} %get-tuple-element.5.res_ref), custom_call_target="tpu_custom_call" | custom-call | tf_op jit(solution)/shard_map/leave/pallas_call | solution.py:555

commit v3 on v2

--- a/solution.py
+++ b/solution.py
@@ -26,7 +26,7 @@
     vel_hbm, forc_hbm, visc_hbm, rp_hbm, gp_hbm, hres_hbm, hval_hbm,
     out_ref, res_ref,
     wide, static, hist, late, ahead, past_res, past_val, coef, first, second, fres, delta,
-    ruler, in_sem, send_sem, recv_sem, gate, *shared,
+    passing, ruler, in_sem, send_sem, recv_sem, gate, *shared,
 ):
     depth, _, cells_x, cells_y, lanes = hres_hbm.shape
     count_x, count_y = counts
@@ -43,12 +43,12 @@
 
     loads = [
         pltpu.make_async_copy(vel_hbm, wide.at[:, HALO : HALO + cells_x, 0:cells_y], in_sem.at[0]),
-        pltpu.make_async_copy(forc_hbm, static.at[0:3, 2 : 2 + cells_x, 0:cells_y], in_sem.at[1]),
-        pltpu.make_async_copy(visc_hbm, static.at[3, 2 : 2 + cells_x, 0:cells_y], in_sem.at[2]),
-        pltpu.make_async_copy(hval_hbm, hist.at[:, :, HALO : HALO + cells_x, 0:cells_y], in_sem.at[3]),
-        pltpu.make_async_copy(hres_hbm, fres, in_sem.at[4]),
-        pltpu.make_async_copy(rp_hbm, past_res, in_sem.at[5]),
-        pltpu.make_async_copy(gp_hbm, past_val, in_sem.at[6]),
+        pltpu.make_async_copy(forc_hbm, static.at[0:3, 2 : 2 + cells_x, 0:cells_y], in_sem.at[0]),
+        pltpu.make_async_copy(visc_hbm, static.at[3, 2 : 2 + cells_x, 0:cells_y], in_sem.at[0]),
+        pltpu.make_async_copy(hval_hbm, hist.at[:, :, HALO : HALO + cells_x, 0:cells_y], in_sem.at[1]),
+        pltpu.make_async_copy(hres_hbm, fres, in_sem.at[2]),
+        pltpu.make_async_copy(rp_hbm, past_res, in_sem.at[2]),
+        pltpu.make_async_copy(gp_hbm, past_val, in_sem.at[2]),
     ]
     for load in loads:
         load.start()
@@ -57,12 +57,14 @@
         pl.semaphore_signal(
             barrier, inc=1, device_id=(me_x, lax.rem(me_y + k, count_y)), device_id_type=MESH
         )
-    for k in range(1, count_x):
-        pl.semaphore_signal(
-            barrier, inc=1, device_id=(lax.rem(me_x + k, count_x), me_y), device_id_type=MESH
-        )
-    total = jnp.int32(count_x + count_y - 2)
-    for sx, sy in DIRS[4:]:
+    for k in range(2, count_x):
+
+        @pl.when(me_x + k < count_x)
+        def _():
+            pl.semaphore_signal(barrier, inc=1, device_id=(me_x + k, me_y), device_id_type=MESH)
+
+    total = count_y - 1 + jnp.maximum(me_x - 1, 0)
+    for sx, sy in DIRS[:2] + DIRS[4:]:
         here = exists(sx, sy)
         total = total + jnp.where(here, 1, 0)
 
@@ -112,16 +114,13 @@
             pieces.append((ref, (sx, sy), 0, span_x(sx, off, deep), span_y(sy, deep)))
         return pieces
 
-    def layers(ref, off, deep, skip):
-        return [(ref, (0, sy), 0, span_x(0, off, 0), span_y(sy, deep, skip)) for sy in (-1, 1)]
-
-    def corners(ref, off):
+    def layer(ref, off, deep, skip, sy):
+        return [(ref, (0, sy), 0, span_x(0, off, 0), span_y(sy, deep, skip))]
+
+    def corners(ref, off, side):
         deep = off - 1
-        pieces = []
-        for sx in (-1, 1):
-            for side, part in ((1, slice(cells_y, cells_y + deep)), (-1, slice(rows - deep, rows))):
-                pieces.append((ref, (sx, 0), side, span_x(sx, off, deep), (part, part)))
-        return pieces
+        part = slice(cells_y, cells_y + deep) if side > 0 else slice(rows - deep, rows)
+        return [(ref, (sx, 0), side, span_x(sx, off, deep), (part, part)) for sx in (-1, 1)]
 
     def length(part):
         return part.stop - part.start
@@ -152,6 +151,9 @@
                     if side != 0:
                         there = there * sides_y[side > 0]
                     size = size + there * size_of(piece)
+                if sending and relayed and sides_y != (1, 1):
+                    near, far = fields["north"][1][0], fields["far"][1][0]
+                    size = size + size_of(near) * (depth - straight) // depth + size_of(far)
                 if size == 0:
                     continue
                 part = ruler.at[0:size]
@@ -173,38 +175,113 @@
                         copy.wait_recv()
 
     fields = {
-        "wide": faces(wide, HALO, DIRS),
-        "static": faces(static, HALO - 1, DIRS),
-        "across": faces(hist, HALO, DIRS[:2]),
-        "near": layers(hist, HALO, HALO - 1, 0),
-        "far": layers(hist, HALO, HALO, HALO - 1),
-        "turn": corners(hist, HALO),
-        "late": faces(late, HALO, DIRS),
+        "wide": (0, faces(wide, HALO, DIRS)),
+        "static": (0, faces(static, HALO - 1, DIRS)),
+        "north": (1, layer(hist, HALO, HALO - 1, 0, -1)),
+        "south": (2, layer(hist, HALO, HALO - 1, 0, 1)),
+        "across": (3, faces(hist, HALO, DIRS[:2])),
+        "far": (3, layer(hist, HALO, HALO, HALO - 1, -1) + layer(hist, HALO, HALO, HALO - 1, 1)),
+        "turn_north": (3, corners(hist, HALO, 1)),
+        "turn_south": (3, corners(hist, HALO, -1)),
+        "late": (3, faces(late, HALO, DIRS)),
     }
-    places_of = {name: n for n, name in enumerate(fields)}
-
-    def send(name):
-        for piece in fields[name]:
-            ref, (sx, sy), side, (src_x, dst_x), (src_y, dst_y) = piece
-            here = exists(sx, sy)
-            if side != 0:
-                here = both(here, exists(0, side))
-            lead = (slice(None),) * (len(ref.shape) - 3)
+    odd = lax.rem(me_y, 2) == 1
+    even = jnp.logical_not(odd)
+
+    relayed = count_y == 4
+    turns = ((1, 1, 3, 2), (-1, 2, 0, 1))
+    bands = {"north": (HALO - 1, 0, 1), "south": (HALO - 1, 0, 1), "far": (HALO, HALO - 1, 0)}
+    straight = depth - (2 * depth) // 5
+
+    def start(name, piece):
+        which = fields[name][0]
+        ref, (sx, sy), side, (src_x, dst_x), (src_y, dst_y) = piece
+        here = exists(sx, sy)
+        if side != 0:
+            here = both(here, exists(0, side))
+        lead = (slice(None),) * (len(ref.shape) - 3)
+
+        def go(lead):
+            pltpu.make_async_remote_copy(
+                src_ref=ref.at[lead + (src_x, src_y)],
+                dst_ref=ref.at[lead + (dst_x, dst_y)],
+                send_sem=send_sem,
+                recv_sem=recv_sem.at[which],
+                device_id=(me_x + sx, me_y + sy),
+                device_id_type=MESH,
+            ).start()
+
+        if relayed and name in bands:
+            turned = me_y == (1 if sy > 0 else 2)
+            if bands[name][2]:
+
+                @pl.when(turned)
+                def _():
+                    go((slice(0, straight), slice(None)))
+
+            here = both(here, jnp.logical_not(turned))
+
+        @pl.when(here)
+        def _():
+            go(lead)
+
+    def passed(name, device, sy, stage):
+        deep, skip, part = bands[name]
+        src_y, dst_y = span_y(sy, deep, skip)
+        group = slice(straight if part else 0, depth)
+        inside = slice(HALO, HALO + cells_x)
+        kept = passing.at[group, :, :, skip:deep]
+        src = hist.at[group, :, inside, src_y] if stage == 0 else kept
+        dst = kept if stage < 2 else hist.at[group, :, inside, dst_y]
+        return pltpu.make_async_remote_copy(
+            src_ref=src,
+            dst_ref=dst,
+            send_sem=send_sem,
+            recv_sem=recv_sem.at[fields[name][0] if stage == 2 else 4 if part else 5],
+            device_id=device,
+            device_id_type=MESH,
+        )
+
+    def detour(names):
+        for name, (sy, owner, relay, _) in zip(names, turns if relayed else ()):
+
+            @pl.when(me_y == owner)
+            def _():
+                passed(name, (me_x, relay), sy, 0).start()
+
+    def pass_on(names):
+        for name, (sy, _, relay, target) in zip(names, turns if relayed else ()):
+
+            @pl.when(me_y == relay)
+            def _():
+                passed(name, (me_x, target), sy, 1).wait_recv()
+                passed(name, (me_x, target), sy, 2).start()
+
+    def send(*names):
+        for name in names:
+            for piece in fields[name][1]:
+                start(name, piece)
+
+    def send_in_turn(*names):
+        for here, first in ((odd, 1), (even, -1)):
 
             @pl.when(here)
             def _():
-                pltpu.make_async_remote_copy(
-                    src_ref=ref.at[lead + (src_x, src_y)],
-                    dst_ref=ref.at[lead + (dst_x, dst_y)],
-                    send_sem=send_sem,
-                    recv_sem=recv_sem.at[places_of[name]],
-                    device_id=(me_x + sx, me_y + sy),
-                    device_id_type=MESH,
-                ).start()
-
-    def receive(name):
-        with jax.named_scope(name):
-            settle(fields[name], recv_sem.at[places_of[name]], False)
+                for sy, kinds in ((first, (1, 0)), (0, (1,)), (-first, (1, 0))):
+                    for kind in kinds:
+                        for name in names:
+                            for piece in fields[name][1]:
+                                if piece[1][1] == sy and (piece[1][0] != 0) == (kind == 1):
+                                    start(name, piece)
+
+    def receive(which):
+        pieces = [p for number, group in fields.values() if number == which for p in group]
+        with jax.named_scope("recv" + str(which)):
+            settle(pieces, recv_sem.at[which], False)
+
+    def turn(which, name):
+        receive(which)
+        send(name)
 
     def along(slots, idx, k, sends, recvs, me, count, axis):
         return pltpu.make_async_remote_copy(
@@ -379,21 +456,37 @@
         for x in range(cells_x):
             relax(lambda c, i: second[c, i + 1], dst, 2, x, cells_y)
 
-    for k in range(1, count_x if direct else 1):
-        pl.semaphore_signal(
-            gate, inc=1, device_id=(lax.rem(me_x + k, count_x), me_y), device_id_type=MESH
-        )
-
-    for load in loads[:3]:
-        load.wait()
-    send("wide")
-    send("static")
-    loads[3].wait()
-    send("near")
-    send("far")
+    if direct:
+        for k in range(1, count_x):
+
+            @pl.when(me_x >= k)
+            def _():
+                pl.semaphore_signal(gate, inc=1, device_id=(me_x - k, me_y), device_id_type=MESH)
+
+        for k in range(1, count_y):
+            pl.semaphore_signal(
+                gate, inc=1, device_id=(me_x, lax.rem(me_y + k, count_y)), device_id_type=MESH
+            )
+
+    def loaded(which, *refs):
+        size = 0
+        for ref in refs:
+            part = 1
+            for extent in ref.shape[:-1]:
+                part = part * extent
+            size = size + part
+        part = ruler.at[0:size]
+        pltpu.make_async_copy(part, part, in_sem.at[which]).wait()
+
+    loaded(0, vel_hbm, forc_hbm, visc_hbm)
+    send_in_turn("wide", "static")
+    loaded(1, hval_hbm)
+    detour(("south", "north"))
+    detour(("far", "far"))
+    send_in_turn("north", "south")
     send("across")
-    for load in loads[4:]:
-        load.wait()
+    send_in_turn("far")
+    loaded(2, hres_hbm, rp_hbm, gp_hbm)
 
     pairs = [(i, j) for i in range(depth) for j in range(i + 1)]
     clear(hist, HALO)
@@ -413,11 +506,11 @@
     row = packed(sums)
     if direct:
         with jax.named_scope("gate"):
-            pl.semaphore_wait(gate, count_x - 1)
+            pl.semaphore_wait(gate, count_x - 1 - me_x + count_y - 1)
     give(0, row)
 
-    receive("wide")
-    receive("static")
+    pass_on(("south", "north"))
+    receive(0)
 
     def store_value(c, x, value):
         late[c, x + HALO, 0:cells_y] = value
@@ -433,9 +526,19 @@
             add(j, fres[j, c, x] * resid)
         add(depth, newest * newest)
     give(1, packed(sums))
-    send("late")
-    receive("near")
-    send("turn")
+    send_in_turn("late")
+    pass_on(("far", "far"))
+
+    @pl.when(odd)
+    def _():
+        turn(1, "turn_north")
+        turn(2, "turn_south")
+
+    @pl.when(even)
+    def _():
+        turn(2, "turn_south")
+        turn(1, "turn_north")
+
     halfway(0)
     halfway(1)
 
@@ -444,8 +547,7 @@
     for n, (i, j) in enumerate(pairs):
         gram[i][j] = gram[j][i] = early[n]
     factors = factored(gram)
-    for name in ("across", "far", "turn", "late"):
-        receive(name)
+    receive(3)
     for_rhs = unpacked(take(1), depth + 1)
     rhs, newest_sq = for_rhs[:depth], for_rhs[depth]
     gamma = solved(factors, rhs)
@@ -489,7 +591,7 @@
         for j in range(1, depth):
             value = value - gamma[j - 1] * hist[j, c, x + HALO, 0:cells_y]
         out_ref[c, x] = value - gamma[depth - 1] * newest
-    pieces = [piece for name in fields for piece in fields[name]]
+    pieces = [piece for _, group in fields.values() for piece in group]
     settle(pieces, send_sem, True, 3 * (count_all - 1) if direct else 0)
     if not direct:
         for line in lines:
@@ -543,10 +645,11 @@
             vmem(3, cells_x + 2, rows),
             vmem(depth, 3, cells_x, cells_y),
             vmem(3, cells_x, cells_y),
+            vmem(depth, 3, cells_x, HALO),
             vmem(length, 1),
-            pltpu.SemaphoreType.DMA((7,)),
+            pltpu.SemaphoreType.DMA((3,)),
             pltpu.SemaphoreType.DMA,
-            pltpu.SemaphoreType.DMA((7,)),
+            pltpu.SemaphoreType.DMA((6,)),
             pltpu.SemaphoreType.REGULAR,
             *shared,
         ],

time: 22.1 us -> 21.4 us (0.968)
  Pallas kernels: 21.3 us -> 20.6 us
    pallas_call x1, Pallas kernels: 20.7 us -> 20 us  [local(): pl.pallas_call(functools.partial(kernel, counts, direct, entries), name='...]
where the time goes in v3:
time: 21.4 us; the launch traced here: 21.3 us
  Pallas kernels  20.6 us (96%)
  between operations  0.64 us (3%)
    pallas_call x1, Pallas kernels, local(): pl.pallas_call(functools.partial(kernel, counts, direct, entries), name='...  20 us
    pallas_call x1, Pallas kernels, local(): pl.pallas_call(leave, name='leave', out_shape=(jax.ShapeDtypeStruct(veloc...  0.66 us

profile of v3, /device:TPU:0, one launch (start us, length us, event | category | flops | bytes accessed | tf_op | source)
XLA Modules:
  0.0 21.3 jit_solution(12440931605996255305)
XLA Ops:
  0.6 20.0 %anderson.1 = (f32[3,4,8,128]{3,2,1,0:T(8,128)S(1)}, f32[3,4,8,128]{3,2,1,0:T(8,128)S(1)}) custom-call(f32[3,4,8,128]{3,2,1,0:T(8,128)} %vel_hbm.1, f32[3,4,8,128]{3,2,1,0:T(8,128)} %forc_hbm.1, f32[4,8,128]{2,1,0:T(8,128)} %visc_hbm.1, f32[3,4,8,128]{3,2,1,0:T(8,128)} %rp_hbm.1, f32[3,4,8,128]{3,2,1,0:T(8,128)} %gp_hbm.1, f32[5,3,4,8,128]{4,3,2,1,0:T(8,128)} %hres_hbm.1, ...), custom_call_target="tpu_custom_call" | custom-call | tf_op jit(solution)/shard_map/anderson/pallas_call | solution.py:629
  20.6 0.7 %leave.1 = (f32[3,4,8,128]{3,2,1,0:T(8,128)}, f32[3,4,8,128]{3,2,1,0:T(8,128)}) custom-call(f32[3,4,8,128]{3,2,1,0:T(8,128)S(1)} %get-tuple-element.4.vel_ref, f32[3,4,8,128]{3,2,1,0:T(8,128)S(1)} %get-tuple-element.5.res_ref), custom_call_target="tpu_custom_call" | custom-call | tf_op jit(solution)/shard_map/leave/pallas_call | solution.py:658

commit v4 on v3

--- a/solution.py
+++ b/solution.py
@@ -50,7 +50,7 @@
         pltpu.make_async_copy(rp_hbm, past_res, in_sem.at[2]),
         pltpu.make_async_copy(gp_hbm, past_val, in_sem.at[2]),
     ]
-    for load in loads:
+    for load in loads[:4]:
         load.start()
     barrier = pltpu.get_barrier_semaphore()
     for k in range(1, count_y):
@@ -191,7 +191,7 @@
     relayed = count_y == 4
     turns = ((1, 1, 3, 2), (-1, 2, 0, 1))
     bands = {"north": (HALO - 1, 0, 1), "south": (HALO - 1, 0, 1), "far": (HALO, HALO - 1, 0)}
-    straight = depth - (2 * depth) // 5
+    straight = depth - (3 * depth) // 5
 
     def start(name, piece):
         which = fields[name][0]
@@ -330,19 +330,33 @@
             total = total + slots[idx, k]
         return total
 
+    def others(me, count):
+        order = []
+        for k in range(count - 1):
+            down = count - 1 - k
+            down = jnp.where(down <= me, down - 1, down)
+            order.append(jnp.where(2 * me < count, down, jnp.where(k >= me, k + 1, k)))
+        return order
+
+    if direct:
+        far_x, far_y = others(me_x, count_x), others(me_y, count_y)
+        ranked = [(kx + 2 * ky, x, y) for kx, x in enumerate(far_x) for ky, y in enumerate(far_y)]
+        ranked += [(kx + 2 * count_y, x, me_y) for kx, x in enumerate(far_x)]
+        ranked += [(count_x + 2 * ky, me_x, y) for ky, y in enumerate(far_y)]
+        peers = [(x, y) for _, x, y in sorted(ranked, key=lambda entry: entry[0])]
+
     def give(idx, row):
         if not direct:
             spread(lines[1], idx, row)
             return
         slots_all[idx, me_all] = row
-        for k in range(1, count_all):
-            peer = lax.rem(me_all + k, count_all)
+        for peer in peers:
             pltpu.make_async_remote_copy(
                 src_ref=slots_all.at[idx, me_all],
                 dst_ref=slots_all.at[idx, me_all],
                 send_sem=send_sem,
                 recv_sem=all_sem.at[idx],
-                device_id=(lax.div(peer, count_y), lax.rem(peer, count_y)),
+                device_id=peer,
                 device_id_type=MESH,
             ).start()
 
@@ -480,12 +494,13 @@
 
     loaded(0, vel_hbm, forc_hbm, visc_hbm)
     send_in_turn("wide", "static")
+    for load in loads[4:]:
+        load.start()
     loaded(1, hval_hbm)
     detour(("south", "north"))
     detour(("far", "far"))
     send_in_turn("north", "south")
     send("across")
-    send_in_turn("far")
     loaded(2, hres_hbm, rp_hbm, gp_hbm)
 
     pairs = [(i, j) for i in range(depth) for j in range(i + 1)]
@@ -526,6 +541,7 @@
             add(j, fres[j, c, x] * resid)
         add(depth, newest * newest)
     give(1, packed(sums))
+    send_in_turn("far")
     send_in_turn("late")
     pass_on(("far", "far"))
 
@@ -583,6 +599,12 @@
     factors = factored(gram2)
 
     halfway(2)
+    pieces = [piece for _, group in fields.values() for piece in group]
+    settle(pieces, send_sem, True, 3 * (count_all - 1) if direct else 0)
+    if not direct:
+        for line in lines:
+            for idx in range(3):
+                whole(line, idx).wait_send()
     final = take(2)
     gamma = solved(factors, unpacked(final, depth))
     for c, x in own:
@@ -591,12 +613,6 @@
         for j in range(1, depth):
             value = value - gamma[j - 1] * hist[j, c, x + HALO, 0:cells_y]
         out_ref[c, x] = value - gamma[depth - 1] * newest
-    pieces = [piece for _, group in fields.values() for piece in group]
-    settle(pieces, send_sem, True, 3 * (count_all - 1) if direct else 0)
-    if not direct:
-        for line in lines:
-            for idx in range(3):
-                whole(line, idx).wait_send()
 
 
 def leave(vel_ref, res_ref, vel_hbm, res_hbm, sem):

time: 21.4 us -> 20.5 us (0.958)
  Pallas kernels: 20.6 us -> 19.7 us
    pallas_call x1, Pallas kernels: 20 us -> 19.1 us  [local(): pl.pallas_call(functools.partial(kernel, counts, direct, entries), name='...]
where the time goes in v4:
time: 20.5 us; the launch traced here: 20.4 us
  Pallas kernels  19.7 us (96%)
  between operations  0.64 us (3%)
    pallas_call x1, Pallas kernels, local(): pl.pallas_call(functools.partial(kernel, counts, direct, entries), name='...  19.1 us
    pallas_call x1, Pallas kernels, local(): pl.pallas_call(leave, name='leave', out_shape=(jax.ShapeDtypeStruct(veloc...  0.66 us

profile of v4, /device:TPU:0, one launch (start us, length us, event | category | flops | bytes accessed | tf_op | source)
XLA Modules:
  0.0 20.4 jit_solution(16828785983160531635)
XLA Ops:
  0.6 19.1 %anderson.1 = (f32[3,4,8,128]{3,2,1,0:T(8,128)S(1)}, f32[3,4,8,128]{3,2,1,0:T(8,128)S(1)}) custom-call(f32[3,4,8,128]{3,2,1,0:T(8,128)} %vel_hbm.1, f32[3,4,8,128]{3,2,1,0:T(8,128)} %forc_hbm.1, f32[4,8,128]{2,1,0:T(8,128)} %visc_hbm.1, f32[3,4,8,128]{3,2,1,0:T(8,128)} %rp_hbm.1, f32[3,4,8,128]{3,2,1,0:T(8,128)} %gp_hbm.1, f32[5,3,4,8,128]{4,3,2,1,0:T(8,128)} %hres_hbm.1, ...), custom_call_target="tpu_custom_call" | custom-call | tf_op jit(solution)/shard_map/anderson/pallas_call | solution.py:645
  19.7 0.7 %leave.1 = (f32[3,4,8,128]{3,2,1,0:T(8,128)}, f32[3,4,8,128]{3,2,1,0:T(8,128)}) custom-call(f32[3,4,8,128]{3,2,1,0:T(8,128)S(1)} %get-tuple-element.4.vel_ref, f32[3,4,8,128]{3,2,1,0:T(8,128)S(1)} %get-tuple-element.5.res_ref), custom_call_target="tpu_custom_call" | custom-call | tf_op jit(solution)/shard_map/leave/pallas_call | solution.py:674

commit v5 on v4

--- a/solution.py
+++ b/solution.py
@@ -191,7 +191,7 @@
     relayed = count_y == 4
     turns = ((1, 1, 3, 2), (-1, 2, 0, 1))
     bands = {"north": (HALO - 1, 0, 1), "south": (HALO - 1, 0, 1), "far": (HALO, HALO - 1, 0)}
-    straight = depth - (3 * depth) // 5
+    straight = depth - (4 * depth) // 5
 
     def start(name, piece):
         which = fields[name][0]
@@ -225,10 +225,13 @@
         def _():
             go(lead)
 
-    def passed(name, device, sy, stage):
+    middle = (straight + depth) // 2
+    groups = {True: (slice(straight, middle), slice(middle, depth)), False: (slice(0, depth),)}
+
+    def passed(name, device, sy, stage, which):
         deep, skip, part = bands[name]
         src_y, dst_y = span_y(sy, deep, skip)
-        group = slice(straight if part else 0, depth)
+        group = groups[part == 1][which]
         inside = slice(HALO, HALO + cells_x)
         kept = passing.at[group, :, :, skip:deep]
         src = hist.at[group, :, inside, src_y] if stage == 0 else kept
@@ -237,7 +240,7 @@
             src_ref=src,
             dst_ref=dst,
             send_sem=send_sem,
-            recv_sem=recv_sem.at[fields[name][0] if stage == 2 else 4 if part else 5],
+            recv_sem=recv_sem.at[fields[name][0] if stage == 2 else 4 + which if part else 6],
             device_id=device,
             device_id_type=MESH,
         )
@@ -247,15 +250,17 @@
 
             @pl.when(me_y == owner)
             def _():
-                passed(name, (me_x, relay), sy, 0).start()
+                for which in range(len(groups[bands[name][2] == 1])):
+                    passed(name, (me_x, relay), sy, 0, which).start()
 
     def pass_on(names):
         for name, (sy, _, relay, target) in zip(names, turns if relayed else ()):
 
             @pl.when(me_y == relay)
             def _():
-                passed(name, (me_x, target), sy, 1).wait_recv()
-                passed(name, (me_x, target), sy, 2).start()
+                for which in range(len(groups[bands[name][2] == 1])):
+                    passed(name, (me_x, target), sy, 1, which).wait_recv()
+                    passed(name, (me_x, target), sy, 2, which).start()
 
     def send(*names):
         for name in names:
@@ -443,30 +448,33 @@
 
     def picard(field, dst):
         for x in range(-2, cells_x + 2):
-            vel = [field[c, x + HALO] for c in range(3)]
-            visc = static[3, x + 2]
+            cut = cells_y if x in (-2, cells_x + 1) else rows
+            vel = [field[c, x + HALO, 0:cut] for c in range(3)]
+            visc = static[3, x + 2, 0:cut]
             diag = 1.0 + 6.0 * visc + jnp.abs(vel[0]) + jnp.abs(vel[1]) + jnp.abs(vel[2])
             inv = 1.0 / diag
             for a in range(3):
                 lo = (visc + jnp.maximum(vel[a], 0.0)) * inv
                 hi = (visc - jnp.minimum(vel[a], 0.0)) * inv
                 if a == 2:
-                    lo, hi = lo * has_below, hi * has_above
-                coef[2 * a, x + 2] = lo
-                coef[2 * a + 1, x + 2] = hi
+                    lo, hi = lo * has_below[0:cut], hi * has_above[0:cut]
+                coef[2 * a, x + 2, 0:cut] = lo
+                coef[2 * a + 1, x + 2, 0:cut] = hi
             for c in range(3):
-                coef[6 + c, x + 2] = (static[c, x + 2] + vel[c]) * inv
+                coef[6 + c, x + 2, 0:cut] = (static[c, x + 2, 0:cut] + vel[c]) * inv
 
         def put(ref, off):
             def store(c, x, value):
-                ref[c, x + off] = value
+                ref[c, x + off, 0 : value.shape[0]] = value
 
             return store
 
         for x in range(-2, cells_x + 2):
-            relax(lambda c, i: field[c, i + HALO], put(first, 2), 2, x, rows)
+            cut = cells_y if x in (-2, cells_x + 1) else rows
+            relax(lambda c, i: field[c, i + HALO], put(first, 2), 2, x, cut)
         for x in range(-1, cells_x + 1):
-            relax(lambda c, i: first[c, i + 2], put(second, 1), 2, x, rows)
+            cut = cells_y if x in (-1, cells_x) else rows
+            relax(lambda c, i: first[c, i + 2], put(second, 1), 2, x, cut)
         for x in range(cells_x):
             relax(lambda c, i: second[c, i + 1], dst, 2, x, cells_y)
 
@@ -519,12 +527,12 @@
         for j in range(depth):
             add(len(pairs) + j, f[j] * r)
     row = packed(sums)
+    pass_on(("south", "north"))
     if direct:
         with jax.named_scope("gate"):
             pl.semaphore_wait(gate, count_x - 1 - me_x + count_y - 1)
     give(0, row)
 
-    pass_on(("south", "north"))
     receive(0)
 
     def store_value(c, x, value):
@@ -541,8 +549,8 @@
             add(j, fres[j, c, x] * resid)
         add(depth, newest * newest)
     give(1, packed(sums))
+    send_in_turn("late")
     send_in_turn("far")
-    send_in_turn("late")
     pass_on(("far", "far"))
 
     @pl.when(odd)
@@ -570,10 +578,11 @@
     wide_gamma = [jnp.concatenate([g, g], 0) for g in gamma]
     for c in range(3):
         for x in range(cells_x + 2 * HALO):
-            value = late[c, x]
+            cut = cells_y if x in (0, cells_x + 2 * HALO - 1) else rows
+            value = late[c, x, 0:cut]
             for j in range(depth):
-                value = value - wide_gamma[j] * hist[j, c, x]
-            ahead[c, x] = value
+                value = value - wide_gamma[j][0:cut] * hist[j, c, x, 0:cut]
+            ahead[c, x, 0:cut] = value
 
     def store_out(c, x, value):
         out_ref[c, x] = value
@@ -665,7 +674,7 @@
             vmem(length, 1),
             pltpu.SemaphoreType.DMA((3,)),
             pltpu.SemaphoreType.DMA,
-            pltpu.SemaphoreType.DMA((6,)),
+            pltpu.SemaphoreType.DMA((7,)),
             pltpu.SemaphoreType.REGULAR,
             *shared,
         ],

time: 20.5 us -> 20.3 us (level)
    pallas_call x1, Pallas kernels: 19.1 us -> 18.9 us  [local(): pl.pallas_call(functools.partial(kernel, counts, direct, entries), name='...]
where the time goes in v5:
time: 20.3 us; the launch traced here: 20.2 us
  Pallas kernels  19.5 us (96%)
  between operations  0.64 us (3%)
    pallas_call x1, Pallas kernels, local(): pl.pallas_call(functools.partial(kernel, counts, direct, entries), name='...  18.9 us
    pallas_call x1, Pallas kernels, local(): pl.pallas_call(leave, name='leave', out_shape=(jax.ShapeDtypeStruct(veloc...  0.66 us

profile of v5, /device:TPU:0, one launch (start us, length us, event | category | flops | bytes accessed | tf_op | source)
XLA Modules:
  0.0 20.2 jit_solution(3496905606720791771)
XLA Ops:
  0.6 18.9 %anderson.1 = (f32[3,4,8,128]{3,2,1,0:T(8,128)S(1)}, f32[3,4,8,128]{3,2,1,0:T(8,128)S(1)}) custom-call(f32[3,4,8,128]{3,2,1,0:T(8,128)} %vel_hbm.1, f32[3,4,8,128]{3,2,1,0:T(8,128)} %forc_hbm.1, f32[4,8,128]{2,1,0:T(8,128)} %visc_hbm.1, f32[3,4,8,128]{3,2,1,0:T(8,128)} %rp_hbm.1, f32[3,4,8,128]{3,2,1,0:T(8,128)} %gp_hbm.1, f32[5,3,4,8,128]{4,3,2,1,0:T(8,128)} %hres_hbm.1, ...), custom_call_target="tpu_custom_call" | custom-call | tf_op jit(solution)/shard_map/anderson/pallas_call | solution.py:654
  19.5 0.7 %leave.1 = (f32[3,4,8,128]{3,2,1,0:T(8,128)}, f32[3,4,8,128]{3,2,1,0:T(8,128)}) custom-call(f32[3,4,8,128]{3,2,1,0:T(8,128)S(1)} %get-tuple-element.4.vel_ref, f32[3,4,8,128]{3,2,1,0:T(8,128)S(1)} %get-tuple-element.5.res_ref), custom_call_target="tpu_custom_call" | custom-call | tf_op jit(solution)/shard_map/leave/pallas_call | solution.py:683

commit v6 on v5

--- a/solution.py
+++ b/solution.py
@@ -338,9 +338,7 @@
     def others(me, count):
         order = []
         for k in range(count - 1):
-            down = count - 1 - k
-            down = jnp.where(down <= me, down - 1, down)
-            order.append(jnp.where(2 * me < count, down, jnp.where(k >= me, k + 1, k)))
+            order.append(jnp.where(k >= me, k + 1, k))
         return order
 
     if direct:
@@ -553,12 +551,14 @@
     send_in_turn("far")
     pass_on(("far", "far"))
 
-    @pl.when(odd)
+    first_north = even if relayed else odd
+
+    @pl.when(first_north)
     def _():
         turn(1, "turn_north")
         turn(2, "turn_south")
 
-    @pl.when(even)
+    @pl.when(jnp.logical_not(first_north))
     def _():
         turn(2, "turn_south")
         turn(1, "turn_north")
@@ -571,10 +571,10 @@
     for n, (i, j) in enumerate(pairs):
         gram[i][j] = gram[j][i] = early[n]
     factors = factored(gram)
-    receive(3)
     for_rhs = unpacked(take(1), depth + 1)
     rhs, newest_sq = for_rhs[:depth], for_rhs[depth]
     gamma = solved(factors, rhs)
+    receive(3)
     wide_gamma = [jnp.concatenate([g, g], 0) for g in gamma]
     for c in range(3):
         for x in range(cells_x + 2 * HALO):

time: 20.3 us -> 20.2 us (level)
  no operation moved by 1% of the time
where the time goes in v6:
time: 20.2 us; the launch traced here: 20 us
  Pallas kernels  19.4 us (96%)
  between operations  0.64 us (3%)
    pallas_call x1, Pallas kernels, local(): pl.pallas_call(functools.partial(kernel, counts, direct, entries), name='...  18.7 us
    pallas_call x1, Pallas kernels, local(): pl.pallas_call(leave, name='leave', out_shape=(jax.ShapeDtypeStruct(veloc...  0.66 us

profile of v6, /device:TPU:0, one launch (start us, length us, event | category | flops | bytes accessed | tf_op | source)
XLA Modules:
  0.0 20.0 jit_solution(11501633895967442731)
XLA Ops:
  0.6 18.7 %anderson.1 = (f32[3,4,8,128]{3,2,1,0:T(8,128)S(1)}, f32[3,4,8,128]{3,2,1,0:T(8,128)S(1)}) custom-call(f32[3,4,8,128]{3,2,1,0:T(8,128)} %vel_hbm.1, f32[3,4,8,128]{3,2,1,0:T(8,128)} %forc_hbm.1, f32[4,8,128]{2,1,0:T(8,128)} %visc_hbm.1, f32[3,4,8,128]{3,2,1,0:T(8,128)} %rp_hbm.1, f32[3,4,8,128]{3,2,1,0:T(8,128)} %gp_hbm.1, f32[5,3,4,8,128]{4,3,2,1,0:T(8,128)} %hres_hbm.1, ...), custom_call_target="tpu_custom_call" | custom-call | tf_op jit(solution)/shard_map/anderson/pallas_call | solution.py:654
  19.4 0.7 %leave.1 = (f32[3,4,8,128]{3,2,1,0:T(8,128)}, f32[3,4,8,128]{3,2,1,0:T(8,128)}) custom-call(f32[3,4,8,128]{3,2,1,0:T(8,128)S(1)} %get-tuple-element.4.vel_ref, f32[3,4,8,128]{3,2,1,0:T(8,128)S(1)} %get-tuple-element.5.res_ref), custom_call_target="tpu_custom_call" | custom-call | tf_op jit(solution)/shard_map/leave/pallas_call | solution.py:683

commit v7 on v6

--- a/solution.py
+++ b/solution.py
@@ -110,8 +110,11 @@
     def faces(ref, off, dirs):
         pieces = []
         for sx, sy in dirs:
-            deep = off if sx == 0 or sy == 0 else off - 1
-            pieces.append((ref, (sx, sy), 0, span_x(sx, off, deep), span_y(sy, deep)))
+            if sx == 0 or sy == 0:
+                pieces.append((ref, (sx, sy), 0, span_x(sx, off, off), span_y(sy, off)))
+            for deep in range(1, off) if sx != 0 and sy != 0 else ():
+                at_x, at_y = span_x(sx, off, deep, deep - 1), span_y(sy, off - deep)
+                pieces.append((ref, (sx, sy), 0, at_x, at_y))
         return pieces
 
     def layer(ref, off, deep, skip, sy):
@@ -267,10 +270,16 @@
             for piece in fields[name][1]:
                 start(name, piece)
 
+    def only(here):
+        def run(body):
+            lax.fori_loop(0, jnp.where(here, 1, 0), lambda i, c: (body(), c)[1], 0)
+
+        return run
+
     def send_in_turn(*names):
         for here, first in ((odd, 1), (even, -1)):
 
-            @pl.when(here)
+            @only(here)
             def _():
                 for sy, kinds in ((first, (1, 0)), (0, (1,)), (-first, (1, 0))):
                     for kind in kinds:
@@ -476,18 +485,6 @@
         for x in range(cells_x):
             relax(lambda c, i: second[c, i + 1], dst, 2, x, cells_y)
 
-    if direct:
-        for k in range(1, count_x):
-
-            @pl.when(me_x >= k)
-            def _():
-                pl.semaphore_signal(gate, inc=1, device_id=(me_x - k, me_y), device_id_type=MESH)
-
-        for k in range(1, count_y):
-            pl.semaphore_signal(
-                gate, inc=1, device_id=(me_x, lax.rem(me_y + k, count_y)), device_id_type=MESH
-            )
-
     def loaded(which, *refs):
         size = 0
         for ref in refs:
@@ -502,6 +499,18 @@
     send_in_turn("wide", "static")
     for load in loads[4:]:
         load.start()
+    if direct:
+        for k in range(1, count_x):
+
+            @pl.when(me_x >= k)
+            def _():
+                pl.semaphore_signal(gate, inc=1, device_id=(me_x - k, me_y), device_id_type=MESH)
+
+        for k in range(1, count_y):
+            pl.semaphore_signal(
+                gate, inc=1, device_id=(me_x, lax.rem(me_y + k, count_y)), device_id_type=MESH
+            )
+
     loaded(1, hval_hbm)
     detour(("south", "north"))
     detour(("far", "far"))
@@ -553,12 +562,12 @@
 
     first_north = even if relayed else odd
 
-    @pl.when(first_north)
+    @only(first_north)
     def _():
         turn(1, "turn_north")
         turn(2, "turn_south")
 
-    @pl.when(jnp.logical_not(first_north))
+    @only(jnp.logical_not(first_north))
     def _():
         turn(2, "turn_south")
         turn(1, "turn_north")

time: 20.2 us -> 20.1 us (level)
  no operation moved by 1% of the time
where the time goes in v7:
time: 20.1 us; the launch traced here: 19.9 us
  Pallas kernels  19.3 us (96%)
  between operations  0.64 us (3%)
    pallas_call x1, Pallas kernels, local(): pl.pallas_call(functools.partial(kernel, counts, direct, entries), name='...  18.6 us
    pallas_call x1, Pallas kernels, local(): pl.pallas_call(leave, name='leave', out_shape=(jax.ShapeDtypeStruct(veloc...  0.66 us

profile of v7, /device:TPU:0, one launch (start us, length us, event | category | flops | bytes accessed | tf_op | source)
XLA Modules:
  0.0 19.9 jit_solution(12166137387647433937)
XLA Ops:
  0.6 18.6 %anderson.1 = (f32[3,4,8,128]{3,2,1,0:T(8,128)S(1)}, f32[3,4,8,128]{3,2,1,0:T(8,128)S(1)}) custom-call(f32[3,4,8,128]{3,2,1,0:T(8,128)} %vel_hbm.1, f32[3,4,8,128]{3,2,1,0:T(8,128)} %forc_hbm.1, f32[4,8,128]{2,1,0:T(8,128)} %visc_hbm.1, f32[3,4,8,128]{3,2,1,0:T(8,128)} %rp_hbm.1, f32[3,4,8,128]{3,2,1,0:T(8,128)} %gp_hbm.1, f32[5,3,4,8,128]{4,3,2,1,0:T(8,128)} %hres_hbm.1, ...), custom_call_target="tpu_custom_call" | custom-call | tf_op jit(solution)/shard_map/anderson/pallas_call | solution.py:663
  19.3 0.7 %leave.1 = (f32[3,4,8,128]{3,2,1,0:T(8,128)}, f32[3,4,8,128]{3,2,1,0:T(8,128)}) custom-call(f32[3,4,8,128]{3,2,1,0:T(8,128)S(1)} %get-tuple-element.4.vel_ref, f32[3,4,8,128]{3,2,1,0:T(8,128)S(1)} %get-tuple-element.5.res_ref), custom_call_target="tpu_custom_call" | custom-call | tf_op jit(solution)/shard_map/leave/pallas_call | solution.py:692

commit v8 on v7

--- a/solution.py
+++ b/solution.py
@@ -344,25 +344,29 @@
             total = total + slots[idx, k]
         return total
 
-    def others(me, count):
+    def others(me, count, upward):
         order = []
         for k in range(count - 1):
-            order.append(jnp.where(k >= me, k + 1, k))
+            up = jnp.where(k >= me, k + 1, k)
+            down = jnp.where(count - 1 - k <= me, count - 2 - k, count - 1 - k)
+            order.append(up if upward else jnp.where(2 * me < count, down, up))
         return order
 
-    if direct:
-        far_x, far_y = others(me_x, count_x), others(me_y, count_y)
+    def ranking(upward):
+        far_x, far_y = others(me_x, count_x, upward), others(me_y, count_y, upward)
         ranked = [(kx + 2 * ky, x, y) for kx, x in enumerate(far_x) for ky, y in enumerate(far_y)]
         ranked += [(kx + 2 * count_y, x, me_y) for kx, x in enumerate(far_x)]
         ranked += [(count_x + 2 * ky, me_x, y) for ky, y in enumerate(far_y)]
-        peers = [(x, y) for _, x, y in sorted(ranked, key=lambda entry: entry[0])]
+        return [(x, y) for _, x, y in sorted(ranked, key=lambda entry: entry[0])]
+
+    peers = [ranking(False), ranking(True)] if direct else None
 
     def give(idx, row):
         if not direct:
             spread(lines[1], idx, row)
             return
         slots_all[idx, me_all] = row
-        for peer in peers:
+        for peer in peers[idx == 2]:
             pltpu.make_async_remote_copy(
                 src_ref=slots_all.at[idx, me_all],
                 dst_ref=slots_all.at[idx, me_all],

time: 20.1 us -> 20 us (level)
  no operation moved by 1% of the time
where the time goes in v8:
time: 20 us; the launch traced here: 19.9 us
  Pallas kernels  19.2 us (96%)
  between operations  0.64 us (3%)
    pallas_call x1, Pallas kernels, local(): pl.pallas_call(functools.partial(kernel, counts, direct, entries), name='...  18.6 us
    pallas_call x1, Pallas kernels, local(): pl.pallas_call(leave, name='leave', out_shape=(jax.ShapeDtypeStruct(veloc...  0.66 us

profile of v8, /device:TPU:0, one launch (start us, length us, event | category | flops | bytes accessed | tf_op | source)
XLA Modules:
  0.0 19.9 jit_solution(11462299771294530911)
XLA Ops:
  0.6 18.6 %anderson.1 = (f32[3,4,8,128]{3,2,1,0:T(8,128)S(1)}, f32[3,4,8,128]{3,2,1,0:T(8,128)S(1)}) custom-call(f32[3,4,8,128]{3,2,1,0:T(8,128)} %vel_hbm.1, f32[3,4,8,128]{3,2,1,0:T(8,128)} %forc_hbm.1, f32[4,8,128]{2,1,0:T(8,128)} %visc_hbm.1, f32[3,4,8,128]{3,2,1,0:T(8,128)} %rp_hbm.1, f32[3,4,8,128]{3,2,1,0:T(8,128)} %gp_hbm.1, f32[5,3,4,8,128]{4,3,2,1,0:T(8,128)} %hres_hbm.1, ...), custom_call_target="tpu_custom_call" | custom-call | tf_op jit(solution)/shard_map/anderson/pallas_call | solution.py:667
  19.2 0.7 %leave.1 = (f32[3,4,8,128]{3,2,1,0:T(8,128)}, f32[3,4,8,128]{3,2,1,0:T(8,128)}) custom-call(f32[3,4,8,128]{3,2,1,0:T(8,128)S(1)} %get-tuple-element.4.vel_ref, f32[3,4,8,128]{3,2,1,0:T(8,128)S(1)} %get-tuple-element.5.res_ref), custom_call_target="tpu_custom_call" | custom-call | tf_op jit(solution)/shard_map/leave/pallas_call | solution.py:696

commit v9 on v8

--- a/solution.py
+++ b/solution.py
@@ -560,8 +560,8 @@
             add(j, fres[j, c, x] * resid)
         add(depth, newest * newest)
     give(1, packed(sums))
+    send_in_turn("far")
     send_in_turn("late")
-    send_in_turn("far")
     pass_on(("far", "far"))
 
     first_north = even if relayed else odd

time: 20 us -> 20 us (level)
  no operation moved by 1% of the time
where the time goes in v9:
time: 20 us; the launch traced here: 19.8 us
  Pallas kernels  19.2 us (96%)
  between operations  0.64 us (3%)
    pallas_call x1, Pallas kernels, local(): pl.pallas_call(functools.partial(kernel, counts, direct, entries), name='...  18.5 us
    pallas_call x1, Pallas kernels, local(): pl.pallas_call(leave, name='leave', out_shape=(jax.ShapeDtypeStruct(veloc...  0.66 us

profile of v9, /device:TPU:0, one launch (start us, length us, event | category | flops | bytes accessed | tf_op | source)
XLA Modules:
  0.0 19.8 jit_solution(13476776815837019235)
XLA Ops:
  0.6 18.5 %anderson.1 = (f32[3,4,8,128]{3,2,1,0:T(8,128)S(1)}, f32[3,4,8,128]{3,2,1,0:T(8,128)S(1)}) custom-call(f32[3,4,8,128]{3,2,1,0:T(8,128)} %vel_hbm.1, f32[3,4,8,128]{3,2,1,0:T(8,128)} %forc_hbm.1, f32[4,8,128]{2,1,0:T(8,128)} %visc_hbm.1, f32[3,4,8,128]{3,2,1,0:T(8,128)} %rp_hbm.1, f32[3,4,8,128]{3,2,1,0:T(8,128)} %gp_hbm.1, f32[5,3,4,8,128]{4,3,2,1,0:T(8,128)} %hres_hbm.1, ...), custom_call_target="tpu_custom_call" | custom-call | tf_op jit(solution)/shard_map/anderson/pallas_call | solution.py:667
  19.2 0.7 %leave.1 = (f32[3,4,8,128]{3,2,1,0:T(8,128)}, f32[3,4,8,128]{3,2,1,0:T(8,128)}) custom-call(f32[3,4,8,128]{3,2,1,0:T(8,128)S(1)} %get-tuple-element.4.vel_ref, f32[3,4,8,128]{3,2,1,0:T(8,128)S(1)} %get-tuple-element.5.res_ref), custom_call_target="tpu_custom_call" | custom-call | tf_op jit(solution)/shard_map/leave/pallas_call | solution.py:696
